TPU v7x, 32 devices: a whole 2x2x4 slice. The times are simulated.
32 devices in a mesh: rep: 2 (over y), shard: 16 (over z, x, core).
Axes of the slice: x: 2, y: 2, z: 4, core: 2. Of those that a mesh axis runs over, the one named last changes fastest.
Arguments:
- activations: bfloat16 [32768, 2048], P(('rep', 'shard')), may hold values from -6 to 6
- cotangents: bfloat16 [32768, 1024], P(('rep', 'shard')), may hold values from -768 to 768
- inner_params: float32 [2, 2048, 1024], P('rep', 'shard'), may hold values from -6 to 6
- inner_moment: float32 [2, 2048, 1024], P('rep', 'shard'), may hold values from 0.25 to 4
- outer_params: float32 [2048, 1024], P('shard'), may hold values from -6 to 6
- momentum: float32 [2048, 1024], P('shard'), may hold values from -3 to 3
Outputs:
- new_params: float32 [2048, 1024], P('shard')
- new_momentum: float32 [2048, 1024], P('shard')
- compute_copy: bfloat16 [2048, 1024], replicated
All inputs are finite; a program needn't handle non-finite values.
Results may differ from a plain program's by a relative error of at most 0.007.
Values may be sent and summed in bfloat16 or wider, within the bound.
No kernel may reach another device: no remote copies, remote signals or barrier semaphores. Data moves between devices by JAX's collectives and lax.ppermute only.
A program may use at most 64 MiB of HBM per device.

v0:
```python
import jax
import jax.numpy as jnp
from jax import lax
from jax.sharding import PartitionSpec as P

outer_rate = 0.7
inertia = 0.9
inner_rate = 0.3
epsilon = 1e-08


def outer_step(pseudo_grad, outer_rows, moment_rows):
    fresh_moment = inertia * moment_rows + pseudo_grad
    fresh_params = outer_rows - outer_rate * (pseudo_grad + inertia * fresh_moment)
    return (fresh_params, fresh_moment)


def per_device(activations, cotangents, inner_params, inner_moment, outer_params, momentum):
    shard_count = lax.axis_size("shard")
    group_count = lax.axis_size("rep")
    group_tok = activations.shape[0] * shard_count
    summed = lax.psum_scatter(
        lax.dot_general(
            activations, cotangents, (((0,), (0,)), ((), ())), preferred_element_type=jnp.float32
        ).astype(jnp.bfloat16),
        "shard",
        scatter_dimension=0,
        tiled=True,
    ).astype(jnp.float32)
    mean_grad = summed / group_tok
    replica_params = inner_params[0] - inner_rate * mean_grad / (
        jnp.sqrt(inner_moment[0]) + epsilon
    )
    param_delta = outer_params - replica_params
    pseudo_grad = lax.psum(param_delta, "rep") / group_count
    new_params, new_momentum = outer_step(pseudo_grad, outer_params, momentum)
    compute_copy = lax.all_gather(new_params.astype(jnp.bfloat16), "shard", axis=0, tiled=True)
    return (new_params, new_momentum, compute_copy)


def solution(mesh):
    in_specs = (
        P(("rep", "shard"), None),
        P(("rep", "shard"), None),
        P("rep", "shard", None),
        P("rep", "shard", None),
        P("shard", None),
        P("shard", None),
    )
    out_specs = (P("shard", None), P("shard", None), P())
    return jax.shard_map(
        per_device, mesh=mesh, in_specs=in_specs, out_specs=out_specs, check_vma=False
    )
```

profile of v0, /device:TPU:0, one launch (start us, length us, event | category | flops | bytes accessed | tf_op | source)
XLA Modules:
  0.0 187.6 jit_solution(9160050818108355666)
XLA Ops:
  7.2 0.0 copy-start
  7.2 0.0 reduce-scatter.2.cloned.1.call-start
  7.2 1.5 copy-done
  8.8 8.3 %convolution_convert_fusion = bf16[2048,1024]{1,0:T(8,128)(2,1)} fusion(bf16[1024,2048]{1,0:T(8,128)(2,1)} %param.6, bf16[1024,1024]{1,0:T(8,128)(2,1)S(1)} %copy-done), kind=kOutput, calls=%fused_computation | convolution fusion | flops 4297064448 | bytes 10485760 | tf_op jit(solution)/shard_map/dot_general | solution.py:23
  17.1 0.0 copy-start.1
  17.1 0.0 copy-start.2
  17.1 0.0 reduce-scatter.2.cloned.1.call-update
  17.1 0.0 all-reduce.2.cloned.1.call-start
  17.1 75.8 %reduce-scatter.2.cloned.1.call-done = bf16[128,1024]{1,0:T(8,128)(2,1)} async-done(((bf16[2048,1024]{1,0:T(8,128)(2,1)}), bf16[128,1024]{1,0:T(8,128)(2,1)}) %reduce-scatter.2.cloned.1.call-update) | async-done | bytes 262160 | tf_op jit(solution)/shard_map/reduce_scatter | solution.py:22
  92.9 0.0 copy-done.1
  92.9 0.0 copy-done.2
  92.9 2.1 %fusion.1 = f32[128,1024]{1,0:T(8,128)} fusion(f32[128,1024]{1,0:T(8,128)S(1)} %copy-done.1, f32[1,128,1024]{2,1,0:T(8,128)S(1)} %copy-done.2, f32[1,128,1024]{2,1,0:T(8,128)} %param.9, bf16[128,1024]{1,0:T(8,128)(2,1)} %reduce-scatter.2.cloned.1.call-done), kind=kLoop, calls=%fused_computation.3 | loop fusion | flops 786432 | bytes 2359296 | tf_op jit(solution)/shard_map/sub | solution.py:34
  95.0 0.0 all-reduce.2.cloned.1.call-update
  95.1 0.0 all-gather.2.cloned.1.call-start
  95.1 28.2 %all-reduce.2.cloned.1.call-done = f32[128,1024]{1,0:T(8,128)} async-done(((f32[128,1024]{1,0:T(8,128)}), f32[128,1024]{1,0:T(8,128)}) %all-reduce.2.cloned.1.call-update) | async-done | bytes 524304 | tf_op jit(solution)/shard_map/psum | solution.py:35
  123.3 2.5 %fusion.2 = (bf16[128,1024]{1,0:T(8,128)(2,1)}, f32[128,1024]{1,0:T(8,128)}, f32[128,1024]{1,0:T(8,128)}) fusion(f32[128,1024]{1,0:T(8,128)S(1)} %copy-done.1, f32[128,1024]{1,0:T(8,128)} %all-reduce.2.cloned.1.call-done, f32[128,1024]{1,0:T(8,128)} %param.11), kind=kLoop, calls=%fused_computation.6 | loop fusion | flops 1048576 | bytes 2883584 | tf_op jit(solution)/shard_map/convert_element_type | solution.py:37
  125.8 0.0 all-gather.2.cloned.1.call-update
  125.8 50.6 %all-gather.2.cloned.1.call-done = bf16[2048,1024]{1,0:T(8,128)(2,1)} async-done(((bf16[128,1024]{1,0:T(8,128)(2,1)}), bf16[2048,1024]{1,0:T(8,128)(2,1)}) %all-gather.2.cloned.1.call-update) | async-done | bytes 4194320 | tf_op jit(solution)/shard_map/all_gather | solution.py:37
  176.5 4.6 %copy.11 = bf16[2048,1024]{1,0:T(8,128)(2,1)} copy(bf16[2048,1024]{1,0:T(8,128)(2,1)} %all-gather.2.cloned.1.call-done) | data formatting | bytes 8388608
Async XLA Ops:
  7.2 1.6 copy-start
  7.2 85.7 %reduce-scatter.2.cloned.1.call-start = ((), (), s32[]{:S(2)}) async-start(), calls=%async_computation.1 | async-start | bytes 4456448 | tf_op jit(solution)/shard_map/reduce_scatter | solution.py:22
  17.1 75.8 %copy-start.1 = (f32[128,1024]{1,0:T(8,128)S(1)}, f32[128,1024]{1,0:T(8,128)}, u32[]{:S(2)}) copy-start(f32[128,1024]{1,0:T(8,128)} %param.10) | copy-start | bytes 1572868
  17.1 75.8 %copy-start.2 = (f32[1,128,1024]{2,1,0:T(8,128)S(1)}, f32[1,128,1024]{2,1,0:T(8,128)}, u32[]{:S(2)}) copy-start(f32[1,128,1024]{2,1,0:T(8,128)} %param.8) | copy-start | bytes 1572868
  17.1 106.2 %all-reduce.2.cloned.1.call-start = ((), (), s32[]{:S(2)}) async-start(), calls=%async_computation.2 | async-start | bytes 1048576 | tf_op jit(solution)/shard_map/psum | solution.py:35
  95.1 81.4 %all-gather.2.cloned.1.call-start = ((), (), s32[]{:S(2)}) async-start(), calls=%async_computation.3 | async-start | bytes 4456448 | tf_op jit(solution)/shard_map/all_gather | solution.py:37
Sparse Core Ops, SparseCore 0:
  17.2 75.6 reduce-scatter.1
  95.7 27.5 all-reduce.1
  126.1 50.3 all-gather.1
where the time goes:
time: 188 us
  waiting for transfers between devices  155 us (82%)
  between operations  13.8 us (7%)
  matrix products  8.29 us (4%)
  local copies, waits for them, and re-layouts  6.19 us (3%)
  other arithmetic  4.62 us (2%)
    reduce_scatter x1, waiting for transfers between devices, per_device(): lax.psum_scatter(lax.dot_general(activations, cotangents, (((0,), (0,)),...  75.8 us
    all_gather x1, waiting for transfers between devices, per_device(): lax.all_gather(new_params.astype(jnp.bfloat16), 'shard', axis=0, tiled=True)  50.6 us
    psum x1, waiting for transfers between devices, per_device(): pseudo_grad = lax.psum(param_delta, 'rep') / group_count  28.2 us
    dot_general x1, matrix products, per_device(): lax.dot_general(activations, cotangents, (((0,), (0,)), ((), ())), prefer...  8.29 us
    unnamed x7, local copies, waits for them, and re-layouts  6.19 us
  transfers between devices with their start and end apart: 3, of which 3 were waited for; matrix products, arithmetic and copies ran while one was open for 0% of the time, Pallas kernels for 0%

commit v1 on v0

--- a/solution.py
+++ b/solution.py
@@ -7,6 +7,12 @@
 inertia = 0.9
 inner_rate = 0.3
 epsilon = 1e-08
+
+
+def gather_and_add(value, mesh_axis):
+    parts = lax.all_gather(value, mesh_axis, axis=0, tiled=False)
+    summed = parts.sum(axis=0)
+    return summed
 
 
 def outer_step(pseudo_grad, outer_rows, moment_rows):
@@ -32,7 +38,7 @@
         jnp.sqrt(inner_moment[0]) + epsilon
     )
     param_delta = outer_params - replica_params
-    pseudo_grad = lax.psum(param_delta, "rep") / group_count
+    pseudo_grad = gather_and_add(param_delta, "rep") / group_count
     new_params, new_momentum = outer_step(pseudo_grad, outer_params, momentum)
     compute_copy = lax.all_gather(new_params.astype(jnp.bfloat16), "shard", axis=0, tiled=True)
     return (new_params, new_momentum, compute_copy)

time: 188 us -> 181 us (0.963)
  waiting for transfers between devices: 155 us -> 147 us
    psum x1 -> x0, waiting for transfers between devices: 28.2 us -> none  [per_device(): pseudo_grad = lax.psum(param_delta, 'rep') / group_count]
    all_gather x0 -> x1, waiting for transfers between devices: none -> 20.3 us  [gather_and_add(): parts = lax.all_gather(value, mesh_axis, axis=0, tiled=False)]
where the time goes in v1:
time: 181 us
  waiting for transfers between devices  147 us (81%)
  between operations  13.8 us (8%)
  matrix products  8.29 us (5%)
  local copies, waits for them, and re-layouts  6.19 us (3%)
  other arithmetic  5.78 us (3%)
    reduce_scatter x1, waiting for transfers between devices, per_device(): lax.psum_scatter(lax.dot_general(activations, cotangents, (((0,), (0,)),...  75.8 us
    all_gather x1, waiting for transfers between devices, per_device(): lax.all_gather(new_params.astype(jnp.bfloat16), 'shard', axis=0, tiled=True)  50.5 us
    all_gather x1, waiting for transfers between devices, gather_and_add(): parts = lax.all_gather(value, mesh_axis, axis=0, tiled=False)  20.3 us
    dot_general x1, matrix products, per_device(): lax.dot_general(activations, cotangents, (((0,), (0,)), ((), ())), prefer...  8.29 us
    unnamed x7, local copies, waits for them, and re-layouts  6.19 us
  transfers between devices with their start and end apart: 3, of which 3 were waited for; matrix products, arithmetic and copies ran while one was open for 0% of the time, Pallas kernels for 0%

profile of v1, /device:TPU:0, one launch (start us, length us, event | category | flops | bytes accessed | tf_op | source)
XLA Modules:
  0.0 180.8 jit_solution(5261960814553591373)
XLA Ops:
  7.2 0.0 copy-start
  7.2 0.0 reduce-scatter.2.cloned.1.call-start
  7.2 1.5 copy-done
  8.8 8.3 %convolution_convert_fusion = bf16[2048,1024]{1,0:T(8,128)(2,1)} fusion(bf16[1024,2048]{1,0:T(8,128)(2,1)} %param.6, bf16[1024,1024]{1,0:T(8,128)(2,1)S(1)} %copy-done), kind=kOutput, calls=%fused_computation | convolution fusion | flops 4297064448 | bytes 10485760 | tf_op jit(solution)/shard_map/dot_general | solution.py:29
  17.1 0.0 copy-start.1
  17.1 0.0 copy-start.2
  17.1 0.0 reduce-scatter.2.cloned.1.call-update
  17.1 0.0 all-gather.6.cloned.1.call-start
  17.1 75.8 %reduce-scatter.2.cloned.1.call-done = bf16[128,1024]{1,0:T(8,128)(2,1)} async-done(((bf16[2048,1024]{1,0:T(8,128)(2,1)}), bf16[128,1024]{1,0:T(8,128)(2,1)}) %reduce-scatter.2.cloned.1.call-update) | async-done | bytes 262160 | tf_op jit(solution)/shard_map/reduce_scatter | solution.py:28
  92.9 0.0 copy-done.1
  92.9 0.0 copy-done.2
  92.9 2.1 %fusion.1 = f32[128,1024]{1,0:T(8,128)} fusion(f32[128,1024]{1,0:T(8,128)S(1)} %copy-done.1, f32[1,128,1024]{2,1,0:T(8,128)S(1)} %copy-done.2, f32[1,128,1024]{2,1,0:T(8,128)} %param.9, bf16[128,1024]{1,0:T(8,128)(2,1)} %reduce-scatter.2.cloned.1.call-done), kind=kLoop, calls=%fused_computation.3 | loop fusion | flops 786432 | bytes 2359296 | tf_op jit(solution)/shard_map/sub | solution.py:40
  95.0 0.0 all-gather.6.cloned.1.call-update
  95.1 0.0 all-gather.4.cloned.1.call-start
  95.1 20.3 %all-gather.6.cloned.1.call-done = f32[256,1024]{1,0:T(8,128)} async-done(((f32[128,1024]{1,0:T(8,128)}), f32[256,1024]{1,0:T(8,128)}) %all-gather.6.cloned.1.call-update) | async-done | bytes 1048592 | tf_op jit(solution)/shard_map/all_gather | solution.py:13
  115.4 1.3 reduce_sum.9
  116.7 2.3 %fusion.2 = (bf16[128,1024]{1,0:T(8,128)(2,1)}, f32[128,1024]{1,0:T(8,128)}, f32[128,1024]{1,0:T(8,128)}) fusion(f32[128,1024]{1,0:T(8,128)S(1)} %copy-done.1, f32[128,1024]{1,0:T(8,128)S(1)} %reduce_sum.9, f32[128,1024]{1,0:T(8,128)} %param.11), kind=kLoop, calls=%fused_computation.6 | loop fusion | flops 1048576 | bytes 2883584 | tf_op jit(solution)/shard_map/convert_element_type | solution.py:43
  119.0 0.0 all-gather.4.cloned.1.call-update
  119.1 50.5 %all-gather.4.cloned.1.call-done = bf16[2048,1024]{1,0:T(8,128)(2,1)} async-done(((bf16[128,1024]{1,0:T(8,128)(2,1)}), bf16[2048,1024]{1,0:T(8,128)(2,1)}) %all-gather.4.cloned.1.call-update) | async-done | bytes 4194320 | tf_op jit(solution)/shard_map/all_gather | solution.py:43
  169.6 4.6 %copy.10 = bf16[2048,1024]{1,0:T(8,128)(2,1)} copy(bf16[2048,1024]{1,0:T(8,128)(2,1)} %all-gather.4.cloned.1.call-done) | data formatting | bytes 8388608
Async XLA Ops:
  7.2 1.6 copy-start
  7.2 85.7 %reduce-scatter.2.cloned.1.call-start = ((), (), s32[]{:S(2)}) async-start(), calls=%async_computation.1 | async-start | bytes 4456448 | tf_op jit(solution)/shard_map/reduce_scatter | solution.py:28
  17.1 75.8 %copy-start.1 = (f32[128,1024]{1,0:T(8,128)S(1)}, f32[128,1024]{1,0:T(8,128)}, u32[]{:S(2)}) copy-start(f32[128,1024]{1,0:T(8,128)} %param.10) | copy-start | bytes 1572868
  17.1 75.8 %copy-start.2 = (f32[1,128,1024]{2,1,0:T(8,128)S(1)}, f32[1,128,1024]{2,1,0:T(8,128)}, u32[]{:S(2)}) copy-start(f32[1,128,1024]{2,1,0:T(8,128)} %param.8) | copy-start | bytes 1572868
  17.1 98.3 %all-gather.6.cloned.1.call-start = ((), (), s32[]{:S(2)}) async-start(), calls=%async_computation.3 | async-start | bytes 1572864 | tf_op jit(solution)/shard_map/all_gather | solution.py:13
  95.1 74.5 %all-gather.4.cloned.1.call-start = ((), (), s32[]{:S(2)}) async-start(), calls=%async_computation.2 | async-start | bytes 4456448 | tf_op jit(solution)/shard_map/all_gather | solution.py:43
Sparse Core Ops, SparseCore 0:
  17.2 75.6 reduce-scatter.1
  95.2 20.1 all-gather.5
  119.2 50.3 all-gather.3
